TPU v7x, 32 devices: a whole 2x2x4 slice. The times are simulated.
32 devices in a mesh: seq: 8 (over y, x, core), exp: 4 (over z).
Axes of the slice: x: 2, y: 2, z: 4, core: 2. Of those that a mesh axis runs over, the one named last changes fastest.
Arguments:
- queries: bfloat16 [8, 512, 512], P(None, 'seq', 'exp'), may hold values from -5 to 5
- keys: bfloat16 [8, 512, 512], P(None, 'seq', 'exp'), may hold values from -5 to 5
- values: bfloat16 [8, 512, 512], P(None, 'seq', 'exp'), may hold values from -170 to 170
- seg_ids: int32 [8, 512], replicated, may hold values from 0 to 3, as said below
- norm_gain: float32 [512], replicated, may hold values from 0.25 to 1.75
- router_w: bfloat16 [512, 16], replicated, may hold values from -0.25 to 0.25
- expert_ids: int32 [512, 8, 1, 2], P(('seq', 'exp')), may hold values from 0 to 15, all different within a row; in each aligned block of 128 rows (0 to 127, 128 to 255, ..., all dimensions but the last counted through in order) at most 32 rows name the same one
- w_in: bfloat16 [16, 512, 1024], P('exp'), may hold values from -0.25 to 0.25
- w_out: bfloat16 [16, 1024, 512], P('exp'), may hold values from -0.1875 to 0.1875
Outputs:
- normed: bfloat16 [8, 512, 512], P(None, ('seq', 'exp'))
- expert_mix: bfloat16 [8, 512, 512], P(None, ('seq', 'exp'))
Inputs may be any that keep to these rules, and one draw needn't show every extreme that they name: `seg_ids`: in each sequence the numbers start at 0, never fall, and rise by one at each of 3 document starts; every start lies at an even position after the middle of the sequence. `expert_ids`: the 2 experts of a sub-token differ. Among the rows of one device (its 16 positions, all sequences, all sub-tokens) no expert is named more than 32 times; in every draw some device names some expert exactly 32 times.
All inputs are finite; a program needn't handle non-finite values.
Results may differ from a plain program's by a relative error of at most 0.015.
Values may be sent and summed in bfloat16 or wider, within the bound.
A program may use at most 128 MiB of HBM per device.

v0:
```python
import functools

import jax
import jax.numpy as jnp
from jax import lax
from jax.experimental import pallas as pl
from jax.experimental.pallas import tpu as pltpu
from jax.sharding import PartitionSpec as P

HD = 128
SUB = 512
TOPK = 2
CAP = 32


NEG = -1e30


def update(running, query_heads, shaped, query_pos, query_seg, key_pos, key_seg, score_scale):
    maxima, totals, running_total = running
    attention_scores = (
        jnp.einsum("bqhd,bkhd->bhqk", query_heads, shaped[0], preferred_element_type=jnp.float32)
        * score_scale
    )
    visible = (key_pos[None, :] <= query_pos[:, None])[None, None] & (
        key_seg[:, None, None, :] == query_seg[:, None, :, None]
    )
    highest = jnp.max(jnp.where(visible, attention_scores, NEG), axis=-1)
    new_max = jnp.maximum(maxima, highest)
    weights = jnp.where(visible, jnp.exp(attention_scores - new_max[..., None]), 0.0)
    rescale_factor = jnp.exp(maxima - new_max)
    totals = totals * rescale_factor + jnp.sum(weights, axis=-1)
    rounded_result = weights.astype(jnp.bfloat16)
    running_total = running_total * rescale_factor[..., None] + jnp.einsum(
        "bhqk,bkhd->bhqd", rounded_result, shaped[1], preferred_element_type=jnp.float32
    )
    return (new_max, totals, running_total)


def attend_block(
    running, query_heads, block, query_pos, query_seg, seg_ids, key_first, score_scale
):
    row_count = block.shape[2]
    key_pos = key_first + jnp.arange(row_count, dtype=jnp.int32)
    key_seg = lax.dynamic_slice_in_dim(seg_ids, key_first, row_count, 1)
    needed = (key_first <= query_pos[-1]) & jnp.any(key_seg[:, -1] >= query_seg[:, 0])
    shaped = block.reshape(2, block.shape[1], row_count, query_heads.shape[2], query_heads.shape[3])
    return lax.cond(
        needed,
        lambda state: update(
            state, query_heads, shaped, query_pos, query_seg, key_pos, key_seg, score_scale
        ),
        lambda state: state,
        running,
    )


def body(queries, keys, values, seg_ids, norm_gain, router_w, expert_ids, w_in, w_out):
    my_index = lax.axis_index("seq")
    seq_count, local_len, local_width = queries.shape
    head_count = local_width // HD
    score_scale = HD ** (-0.5)
    first_pos = my_index * local_len
    query_pos = first_pos + jnp.arange(local_len, dtype=jnp.int32)
    query_seg = lax.dynamic_slice_in_dim(seg_ids, first_pos, local_len, 1)
    query_heads = queries.reshape(seq_count, local_len, head_count, HD)
    initial = (
        jnp.full((seq_count, head_count, local_len), NEG, jnp.float32),
        jnp.zeros((seq_count, head_count, local_len), jnp.float32),
        jnp.zeros((seq_count, head_count, local_len, HD), jnp.float32),
    )
    stacked = jnp.stack([keys, values])

    def attend(running, block, key_first):
        return attend_block(
            running, query_heads, block, query_pos, query_seg, seg_ids, key_first, score_scale
        )

    shard_part = lax.all_gather(stacked, "seq", axis=2, tiled=True)
    row_count = shard_part.shape[2]
    width = min(row_count, local_len)
    repeats = row_count // width

    def inner(number, state):
        section = lax.dynamic_slice_in_dim(shard_part, number * width, width, 2)
        return attend(state, section, number * width)

    running = lax.fori_loop(0, repeats, inner, initial)
    maxima, totals, running_total = running
    attended = (
        (running_total / totals[..., None])
        .transpose(0, 2, 1, 3)
        .reshape(seq_count, local_len, local_width)
        .astype(jnp.bfloat16)
    )
    tokens = lax.all_to_all(attended, "exp", split_axis=1, concat_axis=2, tiled=True)
    values32 = tokens.astype(jnp.float32)
    spread = jnp.sqrt(jnp.mean(values32 * values32, axis=-1, keepdims=True) + 1e-06)
    normed = (values32 / spread * norm_gain).astype(jnp.bfloat16)
    token_count = normed.shape[1]
    feature_count = normed.shape[2]
    sub_count = feature_count // SUB
    sub_rows = (
        normed.reshape(seq_count, token_count, sub_count, SUB)
        .transpose(1, 0, 2, 3)
        .reshape(-1, SUB)
    )
    picks = expert_ids.reshape(-1, TOPK)
    logits = jnp.dot(sub_rows, router_w, preferred_element_type=jnp.float32)
    chosen = jnp.take_along_axis(logits, picks, axis=1)
    sigmas = jax.nn.sigmoid(chosen)
    gates = sigmas / jnp.sum(sigmas, axis=1, keepdims=True)
    expert_total = router_w.shape[1]
    targets = picks.reshape(-1)
    one_hot = (targets[:, None] == jnp.arange(expert_total, dtype=jnp.int32)[None, :]).astype(
        jnp.int32
    )
    earlier = jnp.cumsum(one_hot, axis=0) - one_hot
    slot_rank = jnp.sum(earlier * one_hot, axis=1)
    destination = targets * CAP + slot_rank
    sources = jnp.arange(targets.shape[0], dtype=jnp.int32) // TOPK
    outgoing = (
        jnp.zeros((expert_total * CAP, SUB), jnp.bfloat16)
        .at[destination]
        .set(sub_rows[sources])
        .reshape(expert_total, CAP, SUB)
    )
    arrived = lax.all_to_all(outgoing, "exp", split_axis=0, concat_axis=1, tiled=True)
    hidden = jax.nn.gelu(
        jnp.einsum("ecs,esf->ecf", arrived, w_in, preferred_element_type=jnp.float32),
        approximate=True,
    ).astype(jnp.bfloat16)
    results = jnp.einsum("ecf,efs->ecs", hidden, w_out, preferred_element_type=jnp.float32).astype(
        jnp.bfloat16
    )
    returned = lax.all_to_all(results, "exp", split_axis=1, concat_axis=0, tiled=True).reshape(
        expert_total * CAP, SUB
    )
    picked = returned[destination].reshape(-1, TOPK, SUB).astype(jnp.float32)
    mixed = jnp.sum(gates[:, :, None] * picked, axis=1).astype(jnp.bfloat16)
    expert_mix = mixed.reshape(token_count, seq_count, feature_count).transpose(1, 0, 2)
    return (normed, expert_mix)


MESH = pl.DeviceIdType.MESH


def fused_kernel(
    n_seq, n_exp, per,
    q_ref, k_ref, v_ref, seg_hbm, gain_hbm, router_hbm, ids_hbm, w_in_ref, w_out_ref,
    normed_ref, mix_ref,
    seg_ref, gain_ref, router_ref,
    qkv, att, rows, idsbuf, norm, partial, own_sum, part_out, part_in, win, wout,
    w_sem, qkv_send, qkv_recv, att_send, att_recv, ag_send, ag_recv, ids_send, ids_recv,
    rs_send, rs_recv, relay_in, hop_send, hop_recv, loc_sem,
):
    seqs, local_len, hd = q_ref.shape
    seq_len = n_seq * local_len
    s = lax.axis_index("seq")
    z = lax.axis_index("exp")
    experts_here = w_in_ref.shape[0]
    tok = local_len // n_exp
    width = rows.shape[2]
    groups = seqs // per
    lag = 3
    last = n_exp - 1
    is_end = (z == 0) | (z == last)
    is_mid = (z == 1) | (z == last - 1)
    far = last - z
    near = jnp.where(z <= 1, jnp.where(z == 0, 1, 0), jnp.where(z == last, last - 1, last))
    away = last - near

    small = [
        pltpu.make_async_copy(seg_hbm, seg_ref, loc_sem.at[0]),
        pltpu.make_async_copy(gain_hbm, gain_ref, loc_sem.at[1]),
        pltpu.make_async_copy(router_hbm, router_ref, loc_sem.at[2]),
        pltpu.make_async_copy(ids_hbm, idsbuf.at[z], loc_sem.at[3]),
    ]
    locals_ = [
        pltpu.make_async_copy(
            ref.at[s], qkv.at[i, pl.ds(s * local_len, local_len)], loc_sem.at[5 + i]
        )
        for i, ref in enumerate((q_ref, k_ref, v_ref))
    ]
    w_copies = [
        pltpu.make_async_copy(w_in_ref, win, w_sem.at[0]),
        pltpu.make_async_copy(w_out_ref, wout, w_sem.at[1]),
    ]
    barrier = pltpu.get_barrier_semaphore()
    for d in range(1, n_seq):
        pl.semaphore_signal(
            barrier, inc=1, device_id={"seq": lax.rem(s + d, n_seq), "exp": z}, device_id_type=MESH
        )
    for d in range(1, n_exp):
        pl.semaphore_signal(
            barrier, inc=1, device_id={"seq": s, "exp": lax.rem(z + d, n_exp)}, device_id_type=MESH
        )
    for c in small + locals_:
        c.start()
    pl.semaphore_wait(barrier, n_seq + n_exp - 2)

    copies = []
    for i, ref in enumerate((q_ref, k_ref, v_ref)):
        for d in range(1, n_seq):
            to = lax.rem(s + d, n_seq)
            c = pltpu.make_async_remote_copy(
                src_ref=ref.at[to],
                dst_ref=qkv.at[i, pl.ds(s * local_len, local_len)],
                send_sem=qkv_send.at[i, d],
                recv_sem=qkv_recv.at[i, d],
                device_id={"seq": to, "exp": z},
                device_id_type=MESH,
            )
            c.start()
            copies.append(c)
    id_copies = []
    for d in range(1, n_exp):
        c = pltpu.make_async_remote_copy(
            src_ref=ids_hbm,
            dst_ref=idsbuf.at[z],
            send_sem=ids_send.at[d],
            recv_sem=ids_recv.at[d],
            device_id={"seq": s, "exp": lax.rem(z + d, n_exp)},
            device_id_type=MESH,
        )
        c.start()
        id_copies.append(c)
    for c in w_copies:
        c.start()

    for c in small:
        c.wait()
    seg_row = seg_ref[pl.ds(s, 1), :].astype(jnp.float32)
    seg_cols = jnp.broadcast_to(seg_row, (hd, seq_len)).T

    for c in copies + locals_:
        c.wait()

    step = 128
    scale = hd ** (-0.5)
    for first in range(0, seq_len, step):
        reach = first + step
        scores = lax.dot_general(
            qkv[0, first:reach], qkv[1, :reach], (((1,), (1,)), ((), ())),
            preferred_element_type=jnp.float32,
        ) * scale
        qpos = first + lax.broadcasted_iota(jnp.int32, (step, reach), 0)
        kpos = lax.broadcasted_iota(jnp.int32, (step, reach), 1)
        same = jnp.concatenate(
            [seg_cols[first:reach] == seg_row[:, j:j + step] for j in range(0, reach, step)], axis=1
        )
        visible = (kpos <= qpos) & same
        scores = jnp.where(visible, scores, NEG)
        top = jnp.max(scores, axis=-1, keepdims=True)
        p = jnp.where(visible, jnp.exp(scores - top), 0.0)
        total = jnp.sum(p, axis=-1, keepdims=True)
        o = jnp.dot(p.astype(jnp.bfloat16), qkv[2, :reach], preferred_element_type=jnp.float32)
        att[first:reach] = (o / total).astype(jnp.bfloat16)
    head = pl.ds(pl.multiple_of(z * hd, hd), hd)
    own = pltpu.make_async_copy(
        att.at[pl.ds(s * local_len, local_len)], rows.at[s, :, head], loc_sem.at[4]
    )
    own.start()

    def att_copy(to, source):
        return pltpu.make_async_remote_copy(
            src_ref=att.at[pl.ds(to * local_len, local_len)],
            dst_ref=rows.at[source, :, head],
            send_sem=att_send.at[to],
            recv_sem=att_recv.at[source],
            device_id={"seq": to, "exp": z},
            device_id_type=MESH,
        )

    for d in range(1, n_seq):
        att_copy(lax.rem(s + d, n_seq), s).start()

    def ag_copy(g, d):
        return pltpu.make_async_remote_copy(
            src_ref=rows.at[pl.ds(g * per, per), :, head],
            dst_ref=rows.at[pl.ds(g * per, per), :, head],
            send_sem=ag_send.at[g, d],
            recv_sem=ag_recv.at[g, d],
            device_id={"seq": s, "exp": lax.rem(z + d, n_exp)},
            device_id_type=MESH,
        )

    def ag_arrival(g, d):
        other = lax.rem(z + n_exp - d, n_exp)
        cols = pl.ds(pl.multiple_of(other * hd, hd), hd)
        there = rows.at[pl.ds(g * per, per), :, cols]
        return pltpu.make_async_remote_copy(
            src_ref=there, dst_ref=there, send_sem=ag_send.at[g, d], recv_sem=ag_recv.at[g, d],
            device_id={"seq": s, "exp": other}, device_id_type=MESH,
        )

    def ag_hop(g, owner, to):
        cols = pl.ds(pl.multiple_of(owner * hd, hd), hd)
        there = rows.at[pl.ds(g * per, per), :, cols]
        return pltpu.make_async_remote_copy(
            src_ref=there, dst_ref=there, send_sem=hop_send.at[0, g], recv_sem=hop_recv.at[0, g],
            device_id={"seq": s, "exp": to}, device_id_type=MESH,
        )

    first_group = s // per
    own.wait()
    for i in range(groups):
        g = lax.rem(first_group + i, groups)
        for j in range(per):
            source = g * per + j

            @pl.when(source != s)
            def _():
                att_copy(source, source).wait_recv()

        for d in range(1, n_exp):
            @pl.when(~(is_end & (lax.rem(z + d, n_exp) == far)))
            def _():
                ag_copy(g, d).start()

    for c in id_copies:
        c.wait()
    id_cols = []
    for t in range(TOPK):
        line = jnp.concatenate(
            [idsbuf[e, b, t:t + 1, :] for b in range(seqs) for e in range(n_exp)], axis=1
        ).astype(jnp.float32)
        id_cols.append(jnp.broadcast_to(line, (128, line.shape[1])).T)
    count = per * local_len
    for g in range(groups):
        for t in range(TOPK):
            partial[t, g] = id_cols[t][g * count:(g + 1) * count]
    for c in w_copies:
        c.wait()

    def rs_copy(g, d):
        e = lax.rem(z + d, n_exp)
        return pltpu.make_async_remote_copy(
            src_ref=part_out.at[pl.ds(g * per, per), pl.ds(pl.multiple_of(e * tok, tok), tok), :],
            dst_ref=part_in.at[d, pl.ds(g * per, per)],
            send_sem=rs_send.at[g, d],
            recv_sem=rs_recv.at[g, d],
            device_id={"seq": s, "exp": e},
            device_id_type=MESH,
        )

    def rs_hop(g):
        place = jnp.where(is_end, far, away)
        part = pl.ds(pl.multiple_of(place * tok, tok), tok)
        return pltpu.make_async_remote_copy(
            src_ref=part_out.at[pl.ds(g * per, per), part, :],
            dst_ref=relay_in.at[pl.ds(g * per, per)],
            send_sem=hop_send.at[1, g],
            recv_sem=hop_recv.at[1, g],
            device_id={"seq": s, "exp": near},
            device_id_type=MESH,
        )

    mine = pl.ds(pl.multiple_of(z * tok, tok), tok)

    @pl.loop(0, groups)
    def _(i):
        g = lax.rem(first_group + i, groups)
        members = pl.ds(g * per, per)
        @pl.when(is_mid)
        def _():
            ag_arrival(g, 2).wait_recv()
            ag_hop(g, away, near).start()

        for d in range(1, n_exp):
            held = is_mid if d == 2 else is_end & (lax.rem(z + n_exp - d, n_exp) == far)

            @pl.when(~held)
            def _():
                ag_arrival(g, d).wait_recv()

        @pl.when(is_end)
        def _():
            ag_hop(g, far, near).wait_recv()

        x = rows[members].reshape(count, width).astype(jnp.float32)
        spread = jnp.sqrt(jnp.mean(x * x, axis=-1, keepdims=True) + 1e-06)
        flat = (x / spread * gain_ref[...]).astype(jnp.bfloat16)
        norm[members] = flat.reshape(per, local_len, width)
        logits = lax.dot_general(
            flat, router_ref[...], (((1,), (1,)), ((), ())), preferred_element_type=jnp.float32
        )
        total = logits.shape[1]
        names = lax.broadcasted_iota(jnp.int32, logits.shape, 1).astype(jnp.float32)
        id0, id1 = partial[0, g], partial[1, g]
        c0 = jnp.sum(jnp.where(names == id0[:, :total], logits, 0.0), axis=-1, keepdims=True)
        c1 = jnp.sum(jnp.where(names == id1[:, :total], logits, 0.0), axis=-1, keepdims=True)
        s0 = 1.0 / (1.0 + jnp.exp(-c0))
        s1 = 1.0 / (1.0 + jnp.exp(-c1))
        g0 = s0 / (s0 + s1)
        g1 = s1 / (s0 + s1)
        acc = None
        for j in range(experts_here):
            name = (z * experts_here + j).astype(jnp.float32)
            gate = jnp.where(id0 == name, g0, 0.0) + jnp.where(id1 == name, g1, 0.0)
            u = jnp.dot(flat, win[j], preferred_element_type=jnp.float32)
            act = 0.5 * u * (1.0 + jnp.tanh(0.7978845608028654 * (u + 0.044715 * u * u * u)))
            gates = jnp.concatenate([gate] * (u.shape[1] // gate.shape[1]), axis=1)
            t = jnp.dot(
                (act * gates).astype(jnp.bfloat16), wout[j], preferred_element_type=jnp.float32
            )
            acc = t if acc is None else acc + t
        acc = acc.reshape(per, local_len, width)
        part_out[members] = acc.astype(jnp.bfloat16)
        own_sum[members] = acc
        direct = i >= groups - lag

        @pl.when(is_mid & (i >= lag))
        def _():
            before = lax.rem(first_group + i + groups - lag, groups)
            earlier = pl.ds(before * per, per)
            rs_hop(before).wait_recv()
            part = pl.ds(pl.multiple_of(away * tok, tok), tok)
            both = own_sum[earlier, part, :] + relay_in[earlier].astype(jnp.float32)
            part_out[earlier, part, :] = both.astype(jnp.bfloat16)
            rs_copy(before, lax.rem(away + n_exp - z, n_exp)).start()

        for d in range(1, n_exp):
            e = lax.rem(z + d, n_exp)
            held = ~direct & ((is_end & (e == far)) | (is_mid & (e == away)))

            @pl.when(~held)
            def _():
                rs_copy(g, d).start()

        @pl.when(is_end & ~direct)
        def _():
            rs_hop(g).start()

    normed_ref[...] = norm[:, mine, :]
    for i in range(groups):
        g = lax.rem(first_group + i, groups)
        for d in range(1, n_exp):
            @pl.when(~(is_end & (lax.rem(z + d, n_exp) == far)))
            def _():
                ag_copy(g, d).wait_send()

        @pl.when(is_mid)
        def _():
            ag_hop(g, away, near).wait_send()

        if i < groups - lag:
            @pl.when(is_end)
            def _():
                rs_hop(g).wait_send()

    for d in range(1, n_seq):
        att_copy(lax.rem(s + d, n_seq), s).wait_send()
    for i in range(groups):
        g = lax.rem(first_group + i, groups)
        members = pl.ds(g * per, per)
        acc = own_sum[members, mine, :]
        for d in range(1, n_exp):
            if i >= groups - lag:
                rs_copy(g, d).wait()
                acc = acc + part_in[d, members].astype(jnp.float32)
            else:
                sent = ~(is_end & (lax.rem(z + d, n_exp) == far))
                came = ~(is_end & (lax.rem(z + n_exp - d, n_exp) == far))

                @pl.when(sent)
                def _():
                    rs_copy(g, d).wait_send()

                @pl.when(came)
                def _():
                    rs_copy(g, d).wait_recv()

                @pl.when(~came)
                def _():
                    part_in[d, members] = jnp.zeros((per, tok, width), jnp.bfloat16)

                acc = acc + part_in[d, members].astype(jnp.float32)
        mix_ref[members] = acc.astype(jnp.bfloat16)


def fused_body(n_seq, n_exp, queries, keys, values, seg_ids, norm_gain, router_w, expert_ids, w_in, w_out):
    seqs, local_len, hd = queries.shape
    tok = local_len // n_exp
    per = max(1, 128 // local_len)
    groups = seqs // per
    width = norm_gain.shape[0]
    experts_here, sub, ff = w_in.shape
    ids = expert_ids.reshape(tok, seqs, TOPK).transpose(1, 2, 0)
    bf, f32 = jnp.bfloat16, jnp.float32
    hbm = pl.BlockSpec(memory_space=pltpu.HBM)
    vmem = pl.BlockSpec(memory_space=pltpu.VMEM)
    dma = pltpu.SemaphoreType.DMA
    out = pltpu.VMEM((seqs, tok, width), bf)
    return pl.pallas_call(
        functools.partial(fused_kernel, n_seq, n_exp, per),
        out_shape=(out, out),
        in_specs=[hbm] * 9,
        out_specs=(vmem, vmem),
        scratch_shapes=[
            pltpu.VMEM(seg_ids.shape, jnp.int32),
            pltpu.VMEM((1, width), f32),
            pltpu.VMEM(router_w.shape[::-1], bf),
            pltpu.VMEM((3, n_seq * local_len, hd), bf),
            pltpu.VMEM((n_seq * local_len, hd), bf),
            pltpu.VMEM((seqs, local_len, width), bf),
            pltpu.VMEM((n_exp, seqs, TOPK, tok), jnp.int32),
            pltpu.VMEM((seqs, local_len, width), bf),
            pltpu.VMEM((TOPK, groups, per * local_len, 128), f32),
            pltpu.VMEM((seqs, local_len, width), f32),
            pltpu.VMEM((seqs, local_len, width), bf),
            pltpu.VMEM((n_exp, seqs, tok, width), bf),
            pltpu.VMEM((experts_here, sub, ff), bf),
            pltpu.VMEM((experts_here, ff, sub), bf),
            dma((2,)),
            dma((3, n_seq)), dma((3, n_seq)),
            dma((n_seq,)), dma((n_seq,)),
            dma((groups, n_exp)), dma((groups, n_exp)),
            dma((n_exp,)), dma((n_exp,)),
            dma((groups, n_exp)), dma((groups, n_exp)),
            pltpu.VMEM((seqs, tok, width), bf),
            dma((2, groups)), dma((2, groups)),
            dma((8,)),
        ],
        compiler_params=pltpu.CompilerParams(
            collective_id=0, has_side_effects=True, vmem_limit_bytes=60 * 1024 * 1024
        ),
    )(queries, keys, values, seg_ids, norm_gain.reshape(1, width), router_w.T, ids, w_in, w_out)


def whole_body(n_seq, n_exp, *args):
    queries, norm_gain = args[0], args[4]
    seqs, local_len, width = queries.shape
    fits = (
        seqs == n_seq and width == HD and norm_gain.shape[0] == SUB
        and local_len % (16 * n_exp) == 0 and (local_len * n_seq) % 128 == 0
        and seqs % max(1, 128 // local_len) == 0 and n_exp == 4
    )
    return fused_body(n_seq, n_exp, *args) if fits else body(*args)


def solution(mesh):
    return jax.shard_map(
        functools.partial(whole_body, mesh.shape["seq"], mesh.shape["exp"]),
        mesh=mesh,
        in_specs=(
            P(None, "seq", "exp"),
            P(None, "seq", "exp"),
            P(None, "seq", "exp"),
            P(),
            P(),
            P(),
            P(("seq", "exp"), None, None, None),
            P("exp", None, None),
            P("exp", None, None),
        ),
        out_specs=(P(None, ("seq", "exp"), None), P(None, ("seq", "exp"), None)),
        check_vma=False,
    )
```

profile of v0, /device:TPU:0, one launch (start us, length us, event | category | flops | bytes accessed | tf_op | source)
XLA Modules:
  0.0 38.3 jit_solution(887827678519967476)
XLA Ops:
  0.6 36.3 %shard_map.104 = (bf16[8,16,512]{2,1,0:T(8,128)(2,1)S(1)}, bf16[8,16,512]{2,1,0:T(8,128)(2,1)S(1)}) custom-call(bf16[8,64,128]{2,1,0:T(8,128)(2,1)} %q_ref.1, bf16[8,64,128]{2,1,0:T(8,128)(2,1)} %k_ref.1, bf16[8,64,128]{2,1,0:T(8,128)(2,1)} %v_ref.1, s32[8,512]{1,0:T(8,128)} %seg_hbm.1, f32[1,512]{1,0:T(1,128)} %bitcast.7, bf16[16,512]{1,0:T(8,128)(2,1)} %bitcast.5, ...), custom_call_target="tpu_custom_call" | custom-call | tf_op jit(solution)/shard_map/pallas_call | solution.py:495
  37.0 0.7 %copy.13 = bf16[8,16,512]{2,1,0:T(8,128)(2,1)} copy(bf16[8,16,512]{2,1,0:T(8,128)(2,1)S(1)} %get-tuple-element.2) | data formatting | bytes 262144
  37.6 0.7 %copy.14 = bf16[8,16,512]{2,1,0:T(8,128)(2,1)} copy(bf16[8,16,512]{2,1,0:T(8,128)(2,1)S(1)} %get-tuple-element.3) | data formatting | bytes 262144
where the time goes:
time: 38.4 us; the launch traced here: 38.3 us
  Pallas kernels  36.3 us (95%)
  local copies, waits for them, and re-layouts  1.31 us (3%)
  between operations  0.64 us (2%)
    pallas_call x1, Pallas kernels, fused_body(): pl.pallas_call(functools.partial(fused_kernel, n_seq, n_exp, per), out_sh...  36.3 us
    unnamed x2, local copies, waits for them, and re-layouts  1.31 us

commit v1 on v0

v1 whole, which is shorter than its diff:
```python
import functools

import jax
import jax.numpy as jnp
from jax import lax
from jax.experimental import pallas as pl
from jax.experimental.pallas import tpu as pltpu
from jax.sharding import PartitionSpec as P

HD = 128
SUB = 512
TOPK = 2
CAP = 32


NEG = -1e30


def update(running, query_heads, shaped, query_pos, query_seg, key_pos, key_seg, score_scale):
    maxima, totals, running_total = running
    attention_scores = (
        jnp.einsum("bqhd,bkhd->bhqk", query_heads, shaped[0], preferred_element_type=jnp.float32)
        * score_scale
    )
    visible = (key_pos[None, :] <= query_pos[:, None])[None, None] & (
        key_seg[:, None, None, :] == query_seg[:, None, :, None]
    )
    highest = jnp.max(jnp.where(visible, attention_scores, NEG), axis=-1)
    new_max = jnp.maximum(maxima, highest)
    weights = jnp.where(visible, jnp.exp(attention_scores - new_max[..., None]), 0.0)
    rescale_factor = jnp.exp(maxima - new_max)
    totals = totals * rescale_factor + jnp.sum(weights, axis=-1)
    rounded_result = weights.astype(jnp.bfloat16)
    running_total = running_total * rescale_factor[..., None] + jnp.einsum(
        "bhqk,bkhd->bhqd", rounded_result, shaped[1], preferred_element_type=jnp.float32
    )
    return (new_max, totals, running_total)


def attend_block(
    running, query_heads, block, query_pos, query_seg, seg_ids, key_first, score_scale
):
    row_count = block.shape[2]
    key_pos = key_first + jnp.arange(row_count, dtype=jnp.int32)
    key_seg = lax.dynamic_slice_in_dim(seg_ids, key_first, row_count, 1)
    needed = (key_first <= query_pos[-1]) & jnp.any(key_seg[:, -1] >= query_seg[:, 0])
    shaped = block.reshape(2, block.shape[1], row_count, query_heads.shape[2], query_heads.shape[3])
    return lax.cond(
        needed,
        lambda state: update(
            state, query_heads, shaped, query_pos, query_seg, key_pos, key_seg, score_scale
        ),
        lambda state: state,
        running,
    )


def body(queries, keys, values, seg_ids, norm_gain, router_w, expert_ids, w_in, w_out):
    my_index = lax.axis_index("seq")
    seq_count, local_len, local_width = queries.shape
    head_count = local_width // HD
    score_scale = HD ** (-0.5)
    first_pos = my_index * local_len
    query_pos = first_pos + jnp.arange(local_len, dtype=jnp.int32)
    query_seg = lax.dynamic_slice_in_dim(seg_ids, first_pos, local_len, 1)
    query_heads = queries.reshape(seq_count, local_len, head_count, HD)
    initial = (
        jnp.full((seq_count, head_count, local_len), NEG, jnp.float32),
        jnp.zeros((seq_count, head_count, local_len), jnp.float32),
        jnp.zeros((seq_count, head_count, local_len, HD), jnp.float32),
    )
    stacked = jnp.stack([keys, values])

    def attend(running, block, key_first):
        return attend_block(
            running, query_heads, block, query_pos, query_seg, seg_ids, key_first, score_scale
        )

    shard_part = lax.all_gather(stacked, "seq", axis=2, tiled=True)
    row_count = shard_part.shape[2]
    width = min(row_count, local_len)
    repeats = row_count // width

    def inner(number, state):
        section = lax.dynamic_slice_in_dim(shard_part, number * width, width, 2)
        return attend(state, section, number * width)

    running = lax.fori_loop(0, repeats, inner, initial)
    maxima, totals, running_total = running
    attended = (
        (running_total / totals[..., None])
        .transpose(0, 2, 1, 3)
        .reshape(seq_count, local_len, local_width)
        .astype(jnp.bfloat16)
    )
    tokens = lax.all_to_all(attended, "exp", split_axis=1, concat_axis=2, tiled=True)
    values32 = tokens.astype(jnp.float32)
    spread = jnp.sqrt(jnp.mean(values32 * values32, axis=-1, keepdims=True) + 1e-06)
    normed = (values32 / spread * norm_gain).astype(jnp.bfloat16)
    token_count = normed.shape[1]
    feature_count = normed.shape[2]
    sub_count = feature_count // SUB
    sub_rows = (
        normed.reshape(seq_count, token_count, sub_count, SUB)
        .transpose(1, 0, 2, 3)
        .reshape(-1, SUB)
    )
    picks = expert_ids.reshape(-1, TOPK)
    logits = jnp.dot(sub_rows, router_w, preferred_element_type=jnp.float32)
    chosen = jnp.take_along_axis(logits, picks, axis=1)
    sigmas = jax.nn.sigmoid(chosen)
    gates = sigmas / jnp.sum(sigmas, axis=1, keepdims=True)
    expert_total = router_w.shape[1]
    targets = picks.reshape(-1)
    one_hot = (targets[:, None] == jnp.arange(expert_total, dtype=jnp.int32)[None, :]).astype(
        jnp.int32
    )
    earlier = jnp.cumsum(one_hot, axis=0) - one_hot
    slot_rank = jnp.sum(earlier * one_hot, axis=1)
    destination = targets * CAP + slot_rank
    sources = jnp.arange(targets.shape[0], dtype=jnp.int32) // TOPK
    outgoing = (
        jnp.zeros((expert_total * CAP, SUB), jnp.bfloat16)
        .at[destination]
        .set(sub_rows[sources])
        .reshape(expert_total, CAP, SUB)
    )
    arrived = lax.all_to_all(outgoing, "exp", split_axis=0, concat_axis=1, tiled=True)
    hidden = jax.nn.gelu(
        jnp.einsum("ecs,esf->ecf", arrived, w_in, preferred_element_type=jnp.float32),
        approximate=True,
    ).astype(jnp.bfloat16)
    results = jnp.einsum("ecf,efs->ecs", hidden, w_out, preferred_element_type=jnp.float32).astype(
        jnp.bfloat16
    )
    returned = lax.all_to_all(results, "exp", split_axis=1, concat_axis=0, tiled=True).reshape(
        expert_total * CAP, SUB
    )
    picked = returned[destination].reshape(-1, TOPK, SUB).astype(jnp.float32)
    mixed = jnp.sum(gates[:, :, None] * picked, axis=1).astype(jnp.bfloat16)
    expert_mix = mixed.reshape(token_count, seq_count, feature_count).transpose(1, 0, 2)
    return (normed, expert_mix)


MESH = pl.DeviceIdType.MESH


LAG = 3
RELAY_BOTH = False


def fused_kernel(
    n_seq, n_exp, per,
    q_ref, k_ref, v_ref, seg_hbm, gain_hbm, router_hbm, ids_hbm, w_in_ref, w_out_ref,
    normed_ref, mix_ref,
    seg_ref, gain_ref, router_ref,
    stage, qkv, probs, inverse, att, rows, idsbuf, norm, partial, own_sum, part_out, part_in, relay_in,
    win, wout,
    w_sem, stage_sem, loc_sem, ids_send, ids_recv, qkv_send, qkv_recv, att_send, att_recv,
    ag_send, ag_recv, rs_send, rs_recv, hop_recv,
):
    seqs, local_len, hd = q_ref.shape
    seq_len = n_seq * local_len
    s = lax.axis_index("seq")
    z = lax.axis_index("exp")
    experts_here = w_in_ref.shape[0]
    tok = local_len // n_exp
    width = rows.shape[2]
    groups = seqs // per
    last = n_exp - 1
    is_end = (z == 0) | (z == last)
    is_mid = (z == 1) | (z == last - 1)
    far = last - z
    near = jnp.where(z <= 1, jnp.where(z == 0, 1, 0), jnp.where(z == last, last - 1, last))
    away = last - near
    inner = last - z

    def arrived(ref, sem):
        return pltpu.make_async_remote_copy(
            src_ref=ref, dst_ref=ref, send_sem=sem, recv_sem=sem,
            device_id={"seq": s, "exp": lax.rem(z + 1, n_exp)}, device_id_type=MESH,
        )

    own_pos = pl.ds(s * local_len, local_len)
    barrier = pltpu.get_barrier_semaphore()
    for d in range(1, n_exp):
        pl.semaphore_signal(
            barrier, inc=1, device_id={"seq": s, "exp": lax.rem(z + d, n_exp)}, device_id_type=MESH
        )
    for d in range(1, n_seq):
        pl.semaphore_signal(
            barrier, inc=1, device_id={"seq": lax.rem(s + d, n_seq), "exp": z}, device_id_type=MESH
        )
    sources = (q_ref, k_ref, v_ref)
    staged = [
        pltpu.make_async_copy(ref, stage.at[i], stage_sem) for i, ref in enumerate(sources)
    ]
    small = [
        pltpu.make_async_copy(seg_hbm, seg_ref, loc_sem.at[0]),
        pltpu.make_async_copy(gain_hbm, gain_ref, loc_sem.at[1]),
        pltpu.make_async_copy(router_hbm, router_ref, loc_sem.at[2]),
    ]
    locals_ = [
        pltpu.make_async_copy(ref.at[s], qkv.at[i, own_pos], qkv_recv.at[i // 2])
        for i, ref in enumerate(sources)
    ]
    own_ids = pltpu.make_async_copy(ids_hbm, idsbuf.at[z], ids_recv)
    w_copies = [
        pltpu.make_async_copy(w_in_ref, win, w_sem.at[0]),
        pltpu.make_async_copy(w_out_ref, wout, w_sem.at[1]),
    ]
    for c in staged + small + locals_ + [own_ids]:
        c.start()
    arrived(stage, stage_sem).wait_recv()
    pl.semaphore_wait(barrier, n_seq + n_exp - 2)

    for i in range(3):
        for d in range(1, n_seq):
            to = lax.rem(s + d, n_seq)
            pltpu.make_async_remote_copy(
                src_ref=stage.at[i, to],
                dst_ref=qkv.at[i, own_pos],
                send_sem=qkv_send,
                recv_sem=qkv_recv.at[i // 2],
                device_id={"seq": to, "exp": z},
                device_id_type=MESH,
            ).start()
    for d in range(1, n_exp):
        pltpu.make_async_remote_copy(
            src_ref=ids_hbm,
            dst_ref=idsbuf.at[z],
            send_sem=ids_send,
            recv_sem=ids_recv,
            device_id={"seq": s, "exp": lax.rem(z + d, n_exp)},
            device_id_type=MESH,
        ).start()
    for c in w_copies:
        c.start()

    for c in small:
        c.wait()
    seg_row = seg_ref[pl.ds(s, 1), :].astype(jnp.float32)
    seg_cols = jnp.broadcast_to(seg_row, (hd, seq_len)).T

    arrived(idsbuf, ids_recv).wait_recv()
    count = per * local_len
    for t in range(TOPK):
        line = jnp.concatenate(
            [idsbuf[e, b, t:t + 1, :] for b in range(seqs) for e in range(n_exp)], axis=1
        ).astype(jnp.float32)
        cols = jnp.broadcast_to(line, (128, line.shape[1])).T
        for g in range(groups):
            partial[t, g] = cols[g * count:(g + 1) * count]

    arrived(qkv.at[pl.ds(0, 2)], qkv_recv.at[0]).wait_recv()
    step = 128
    scale = hd ** (-0.5) * 1.4426950408889634
    for first in range(0, seq_len, step):
        reach = first + step
        scores = lax.dot_general(
            qkv[0, first:reach], qkv[1, :reach], (((1,), (1,)), ((), ())),
            preferred_element_type=jnp.float32,
        )
        qpos = first + lax.broadcasted_iota(jnp.int32, (step, reach), 0)
        kpos = lax.broadcasted_iota(jnp.int32, (step, reach), 1)
        same = jnp.concatenate(
            [seg_cols[first:reach] == seg_row[:, j:j + step] for j in range(0, reach, step)], axis=1
        )
        scores = jnp.where((kpos <= qpos) & same, scores, NEG)
        top = jnp.max(scores, axis=-1, keepdims=True)
        p = jnp.exp2((scores - top) * scale)
        total = jnp.sum(p, axis=-1, keepdims=True)
        probs[first:reach, :reach] = p.astype(jnp.bfloat16)
        inverse[first:reach, :] = jnp.broadcast_to(1.0 / total, (step, hd))
    arrived(qkv.at[2], qkv_recv.at[1]).wait_recv()
    for first in range(0, seq_len, step):
        reach = first + step
        o = jnp.dot(
            probs[first:reach, :reach], qkv[2, :reach], preferred_element_type=jnp.float32
        )
        att[first:reach] = (o * inverse[first:reach]).astype(jnp.bfloat16)

    head = pl.ds(pl.multiple_of(z * hd, hd), hd)
    first_group = s // per
    pltpu.make_async_copy(att.at[own_pos], rows.at[s, :, head], att_recv.at[first_group]).start()
    for d in range(1, n_seq):
        to = lax.rem(s + d, n_seq)
        pltpu.make_async_remote_copy(
            src_ref=att.at[pl.ds(to * local_len, local_len)],
            dst_ref=rows.at[s, :, head],
            send_sem=att_send,
            recv_sem=att_recv.at[first_group],
            device_id={"seq": to, "exp": z},
            device_id_type=MESH,
        ).start()

    def ag_copy(g, owner, to):
        cols = pl.ds(pl.multiple_of(owner * hd, hd), hd)
        there = rows.at[pl.ds(g * per, per), :, cols]
        return pltpu.make_async_remote_copy(
            src_ref=there, dst_ref=there, send_sem=ag_send, recv_sem=ag_recv.at[g],
            device_id={"seq": s, "exp": to}, device_id_type=MESH,
        )

    for i in range(groups):
        g = lax.rem(first_group + i, groups)
        arrived(rows.at[pl.ds(g * per, per), :, head], att_recv.at[g]).wait_recv()
        for d in range(1, n_exp):
            e = lax.rem(z + d, n_exp)
            held = is_end & (e == far)
            if RELAY_BOTH:
                held = held | (is_mid & (e == away))

            @pl.when(~held)
            def _():
                ag_copy(g, z, e).start()

    for c in w_copies:
        c.wait()

    def rs_copy(g, d):
        e = lax.rem(z + d, n_exp)
        return pltpu.make_async_remote_copy(
            src_ref=part_out.at[pl.ds(g * per, per), pl.ds(pl.multiple_of(e * tok, tok), tok), :],
            dst_ref=part_in.at[d, pl.ds(g * per, per)],
            send_sem=rs_send,
            recv_sem=rs_recv.at[g],
            device_id={"seq": s, "exp": e},
            device_id_type=MESH,
        )

    def rs_hop(g):
        place = jnp.where(is_end, far, away)
        part = pl.ds(pl.multiple_of(place * tok, tok), tok)
        return pltpu.make_async_remote_copy(
            src_ref=part_out.at[pl.ds(g * per, per), part, :],
            dst_ref=relay_in.at[pl.ds(g * per, per)],
            send_sem=rs_send,
            recv_sem=hop_recv.at[g],
            device_id={"seq": s, "exp": near},
            device_id_type=MESH,
        )

    mine = pl.ds(pl.multiple_of(z * tok, tok), tok)

    def pass_on(before):
        earlier = pl.ds(before * per, per)
        rs_hop(before).wait_recv()
        part = pl.ds(pl.multiple_of(away * tok, tok), tok)
        both = own_sum[earlier, part, :] + relay_in[earlier].astype(jnp.float32)
        part_out[earlier, part, :] = both.astype(jnp.bfloat16)
        rs_copy(before, lax.rem(away + n_exp - z, n_exp)).start()

    @pl.loop(0, groups)
    def _(i):
        g = lax.rem(first_group + i, groups)
        members = pl.ds(g * per, per)
        arrived(rows.at[members, :, pl.ds(0, width - hd)], ag_recv.at[g]).wait_recv()

        @pl.when(is_mid)
        def _():
            if RELAY_BOTH:
                ag_copy(g, inner, near).start()
            ag_copy(g, away, near).start()

        x = rows[members].reshape(count, width).astype(jnp.float32)
        inv = 1.0 / jnp.sqrt(jnp.mean(x * x, axis=-1, keepdims=True) + 1e-06)
        flat = (x * inv * gain_ref[...]).astype(jnp.bfloat16)
        norm[members] = flat.reshape(per, local_len, width)
        logits = lax.dot_general(
            flat, router_ref[...], (((1,), (1,)), ((), ())), preferred_element_type=jnp.float32
        )
        total = logits.shape[1]
        names = lax.broadcasted_iota(jnp.int32, logits.shape, 1).astype(jnp.float32)
        id0, id1 = partial[0, g], partial[1, g]
        c0 = jnp.sum(jnp.where(names == id0[:, :total], logits, 0.0), axis=-1, keepdims=True)
        c1 = jnp.sum(jnp.where(names == id1[:, :total], logits, 0.0), axis=-1, keepdims=True)
        s0 = 1.0 / (1.0 + jnp.exp(-c0))
        s1 = 1.0 / (1.0 + jnp.exp(-c1))
        half = 0.5 / (s0 + s1)
        g0 = s0 * half
        g1 = s1 * half
        acc = None
        for j in range(experts_here):
            name = (z * experts_here + j).astype(jnp.float32)
            gate = jnp.where(id0 == name, g0, 0.0) + jnp.where(id1 == name, g1, 0.0)
            u = jnp.dot(flat, win[j], preferred_element_type=jnp.float32)
            bent = jnp.tanh(u * (0.7978845608028654 + 0.035677408136300125 * (u * u)))
            scaled = u * jnp.concatenate([gate] * (u.shape[1] // gate.shape[1]), axis=1)
            t = jnp.dot(
                (scaled + scaled * bent).astype(jnp.bfloat16), wout[j],
                preferred_element_type=jnp.float32,
            )
            acc = t if acc is None else acc + t
        acc = acc.reshape(per, local_len, width)
        part_out[members] = acc.astype(jnp.bfloat16)
        own_sum[members] = acc
        direct = i >= groups - LAG

        @pl.when(is_mid & (i >= LAG))
        def _():
            pass_on(lax.rem(first_group + i + groups - LAG, groups))

        for d in range(1, n_exp):
            e = lax.rem(z + d, n_exp)
            held = ~direct & ((is_end & (e == far)) | (is_mid & (e == away)))

            @pl.when(~held)
            def _():
                rs_copy(g, d).start()

        @pl.when(is_end & ~direct)
        def _():
            rs_hop(g).start()

    normed_ref[...] = norm[:, mine, :]
    for i in range(groups):
        g = lax.rem(first_group + i, groups)
        members = pl.ds(g * per, per)
        acc = own_sum[members, mine, :]
        if i >= groups - LAG:
            arrived(part_in.at[pl.ds(0, n_exp - 1), members], rs_recv.at[g]).wait_recv()
        else:
            @pl.when(is_end)
            def _():
                lost = lax.rem(z + n_exp - far, n_exp)
                arrived(part_in.at[pl.ds(0, n_exp - 2), members], rs_recv.at[g]).wait_recv()
                part_in[lost, members] = jnp.zeros((per, tok, width), jnp.bfloat16)

            @pl.when(~is_end)
            def _():
                arrived(part_in.at[pl.ds(0, n_exp - 1), members], rs_recv.at[g]).wait_recv()

        for d in range(1, n_exp):
            acc = acc + part_in[d, members].astype(jnp.float32)
        mix_ref[members] = acc.astype(jnp.bfloat16)

    def sent(ref, sem):
        arrived(ref, sem).wait_send()

    sent(qkv.at[:, pl.ds(0, seq_len - local_len)], qkv_send)
    sent(att.at[pl.ds(0, seq_len - local_len)], att_send)
    sent(idsbuf.at[pl.ds(0, n_exp - 1)], ids_send)
    sent(part_out.at[:, pl.ds(0, local_len - tok), :], rs_send)

    @pl.when(is_mid)
    def _():
        sent(rows, ag_send)

    @pl.when(~is_mid)
    def _():
        sent(rows.at[:, :, pl.ds(0, (n_exp - 2) * hd)], ag_send)


def move_kernel(a_ref, b_ref, to_a, to_b, sems):
    first = pltpu.make_async_copy(a_ref, to_a, sems.at[0])
    second = pltpu.make_async_copy(b_ref, to_b, sems.at[1])
    first.start()
    second.start()
    first.wait()
    second.wait()


def fused_body(n_seq, n_exp, queries, keys, values, seg_ids, norm_gain, router_w, expert_ids, w_in, w_out):
    seqs, local_len, hd = queries.shape
    tok = local_len // n_exp
    per = max(1, 128 // local_len)
    groups = seqs // per
    width = norm_gain.shape[0]
    experts_here, sub, ff = w_in.shape
    seq_len = n_seq * local_len
    ids = expert_ids.reshape(tok, seqs, TOPK).transpose(1, 2, 0)
    bf, f32 = jnp.bfloat16, jnp.float32
    hbm = pl.BlockSpec(memory_space=pltpu.HBM)
    vmem = pl.BlockSpec(memory_space=pltpu.VMEM)
    dma = pltpu.SemaphoreType.DMA
    out = pltpu.VMEM((seqs, tok, width), bf)
    normed, mix = pl.pallas_call(
        functools.partial(fused_kernel, n_seq, n_exp, per),
        out_shape=(out, out),
        in_specs=[hbm] * 9,
        out_specs=(vmem, vmem),
        scratch_shapes=[
            pltpu.VMEM(seg_ids.shape, jnp.int32),
            pltpu.VMEM((1, width), f32),
            pltpu.VMEM(router_w.shape[::-1], bf),
            pltpu.VMEM((3, seqs, local_len, hd), bf),
            pltpu.VMEM((3, seq_len, hd), bf),
            pltpu.VMEM((seq_len, seq_len), bf),
            pltpu.VMEM((seq_len, hd), f32),
            pltpu.VMEM((seq_len, hd), bf),
            pltpu.VMEM((seqs, local_len, width), bf),
            pltpu.VMEM((n_exp, seqs, TOPK, tok), jnp.int32),
            pltpu.VMEM((seqs, local_len, width), bf),
            pltpu.VMEM((TOPK, groups, per * local_len, 128), f32),
            pltpu.VMEM((seqs, local_len, width), f32),
            pltpu.VMEM((seqs, local_len, width), bf),
            pltpu.VMEM((n_exp, seqs, tok, width), bf),
            pltpu.VMEM((seqs, tok, width), bf),
            pltpu.VMEM((experts_here, sub, ff), bf),
            pltpu.VMEM((experts_here, ff, sub), bf),
            dma((2,)), dma(()), dma((3,)), dma(()), dma(()), dma(()), dma((2,)), dma(()), dma((groups,)),
            dma(()), dma((groups,)), dma(()), dma((groups,)), dma((groups,)),
        ],
        compiler_params=pltpu.CompilerParams(
            collective_id=0, has_side_effects=True, vmem_limit_bytes=60 * 1024 * 1024
        ),
    )(queries, keys, values, seg_ids, norm_gain.reshape(1, width), router_w.T, ids, w_in, w_out)
    result = jax.ShapeDtypeStruct((seqs, tok, width), bf)
    return pl.pallas_call(
        move_kernel,
        out_shape=(result, result),
        in_specs=[pl.BlockSpec(memory_space=pl.ANY)] * 2,
        out_specs=(hbm, hbm),
        scratch_shapes=[dma((2,))],
        compiler_params=pltpu.CompilerParams(vmem_limit_bytes=1024 * 1024),
    )(normed, mix)


def whole_body(n_seq, n_exp, *args):
    queries, norm_gain = args[0], args[4]
    seqs, local_len, width = queries.shape
    fits = (
        seqs == n_seq and width == HD and norm_gain.shape[0] == SUB
        and local_len % (16 * n_exp) == 0 and (local_len * n_seq) % 128 == 0
        and seqs % max(1, 128 // local_len) == 0 and n_exp == 4
    )
    return fused_body(n_seq, n_exp, *args) if fits else body(*args)


def solution(mesh):
    return jax.shard_map(
        functools.partial(whole_body, mesh.shape["seq"], mesh.shape["exp"]),
        mesh=mesh,
        in_specs=(
            P(None, "seq", "exp"),
            P(None, "seq", "exp"),
            P(None, "seq", "exp"),
            P(),
            P(),
            P(),
            P(("seq", "exp"), None, None, None),
            P("exp", None, None),
            P("exp", None, None),
        ),
        out_specs=(P(None, ("seq", "exp"), None), P(None, ("seq", "exp"), None)),
        check_vma=False,
    )
```

time: 38.4 us -> 35.5 us (0.924)
  Pallas kernels: 36.3 us -> 34.8 us
  local copies, waits for them, and re-layouts: 1.31 us -> 0 us
    pallas_call x1, Pallas kernels: 36.3 us -> 34 us  [fused_body(): pl.pallas_call(functools.partial(fused_kernel, n_seq, n_exp, per), out_sh...]
    unnamed x2 -> x0, local copies, waits for them, and re-layouts: 1.31 us -> none
    pallas_call x0 -> x1, Pallas kernels: none -> 0.72 us  [fused_body(): pl.pallas_call(move_kernel, out_shape=(result, result), in_specs=[pl.Bloc...]
where the time goes in v1:
time: 35.5 us; the launch traced here: 35.4 us
  Pallas kernels  34.8 us (98%)
  between operations  0.64 us (2%)
    pallas_call x1, Pallas kernels, fused_body(): pl.pallas_call(functools.partial(fused_kernel, n_seq, n_exp, per), out_sh...  34 us
    pallas_call x1, Pallas kernels, fused_body(): pl.pallas_call(move_kernel, out_shape=(result, result), in_specs=[pl.Bloc...  0.72 us

profile of v1, /device:TPU:0, one launch (start us, length us, event | category | flops | bytes accessed | tf_op | source)
XLA Modules:
  0.0 35.4 jit_solution(11622640940530643049)
XLA Ops:
  0.6 34.0 %shard_map.104 = (bf16[8,16,512]{2,1,0:T(8,128)(2,1)S(1)}, bf16[8,16,512]{2,1,0:T(8,128)(2,1)S(1)}) custom-call(bf16[8,64,128]{2,1,0:T(8,128)(2,1)} %q_ref.1, bf16[8,64,128]{2,1,0:T(8,128)(2,1)} %k_ref.1, bf16[8,64,128]{2,1,0:T(8,128)(2,1)} %v_ref.1, s32[8,512]{1,0:T(8,128)} %seg_hbm.1, f32[1,512]{1,0:T(1,128)} %bitcast.7, bf16[16,512]{1,0:T(8,128)(2,1)} %bitcast.5, ...), custom_call_target="tpu_custom_call" | custom-call | tf_op jit(solution)/shard_map/pallas_call | solution.py:478
  34.7 0.7 %shard_map.105 = (bf16[8,16,512]{2,1,0:T(8,128)(2,1)}, bf16[8,16,512]{2,1,0:T(8,128)(2,1)}) custom-call(bf16[8,16,512]{2,1,0:T(8,128)(2,1)S(1)} %get-tuple-element.4.a_ref, bf16[8,16,512]{2,1,0:T(8,128)(2,1)S(1)} %get-tuple-element.5.b_ref), custom_call_target="tpu_custom_call" | custom-call | tf_op jit(solution)/shard_map/pallas_call | solution.py:510

commit v2 on v1

--- a/solution.py
+++ b/solution.py
@@ -145,8 +145,9 @@
 MESH = pl.DeviceIdType.MESH
 
 
-LAG = 3
-RELAY_BOTH = False
+RELAYED = 2
+CHUNK = 256
+AHEAD = 1
 
 
 def fused_kernel(
@@ -154,10 +155,10 @@
     q_ref, k_ref, v_ref, seg_hbm, gain_hbm, router_hbm, ids_hbm, w_in_ref, w_out_ref,
     normed_ref, mix_ref,
     seg_ref, gain_ref, router_ref,
-    stage, qkv, probs, inverse, att, rows, idsbuf, norm, partial, own_sum, part_out, part_in, relay_in,
-    win, wout,
+    stage, qkv, probs, inverse, att, rows, idsbuf, partial, own_sum, part_out, part_in, relay_in,
+    hidden, win, wout,
     w_sem, stage_sem, loc_sem, ids_send, ids_recv, qkv_send, qkv_recv, att_send, att_recv,
-    ag_send, ag_recv, rs_send, rs_recv, hop_recv,
+    ag_send, far_send, ag_recv, rs_send, rs_recv, hop_recv,
 ):
     seqs, local_len, hd = q_ref.shape
     seq_len = n_seq * local_len
@@ -173,13 +174,19 @@
     far = last - z
     near = jnp.where(z <= 1, jnp.where(z == 0, 1, 0), jnp.where(z == last, last - 1, last))
     away = last - near
-    inner = last - z
 
     def arrived(ref, sem):
         return pltpu.make_async_remote_copy(
             src_ref=ref, dst_ref=ref, send_sem=sem, recv_sem=sem,
             device_id={"seq": s, "exp": lax.rem(z + 1, n_exp)}, device_id_type=MESH,
         )
+
+    chip = s // 2
+    if n_seq == 8:
+        chips = (3 - chip, lax.rem(chip + 2, 4), chip + 1 - 2 * lax.rem(chip, 2))
+        peers = [2 * c + k for c in chips for k in range(2)] + [s + 1 - 2 * lax.rem(s, 2)]
+    else:
+        peers = [lax.rem(s + d, n_seq) for d in range(1, n_seq)]
 
     own_pos = pl.ds(s * local_len, local_len)
     barrier = pltpu.get_barrier_semaphore()
@@ -215,8 +222,7 @@
     pl.semaphore_wait(barrier, n_seq + n_exp - 2)
 
     for i in range(3):
-        for d in range(1, n_seq):
-            to = lax.rem(s + d, n_seq)
+        for to in peers:
             pltpu.make_async_remote_copy(
                 src_ref=stage.at[i, to],
                 dst_ref=qkv.at[i, own_pos],
@@ -283,8 +289,7 @@
     head = pl.ds(pl.multiple_of(z * hd, hd), hd)
     first_group = s // per
     pltpu.make_async_copy(att.at[own_pos], rows.at[s, :, head], att_recv.at[first_group]).start()
-    for d in range(1, n_seq):
-        to = lax.rem(s + d, n_seq)
+    for to in peers[-1:] + peers[:-1]:
         pltpu.make_async_remote_copy(
             src_ref=att.at[pl.ds(to * local_len, local_len)],
             dst_ref=rows.at[s, :, head],
@@ -294,11 +299,11 @@
             device_id_type=MESH,
         ).start()
 
-    def ag_copy(g, owner, to):
+    def ag_copy(g, owner, to, sem):
         cols = pl.ds(pl.multiple_of(owner * hd, hd), hd)
         there = rows.at[pl.ds(g * per, per), :, cols]
         return pltpu.make_async_remote_copy(
-            src_ref=there, dst_ref=there, send_sem=ag_send, recv_sem=ag_recv.at[g],
+            src_ref=there, dst_ref=there, send_sem=sem, recv_sem=ag_recv.at[g],
             device_id={"seq": s, "exp": to}, device_id_type=MESH,
         )
 
@@ -307,13 +312,9 @@
         arrived(rows.at[pl.ds(g * per, per), :, head], att_recv.at[g]).wait_recv()
         for d in range(1, n_exp):
             e = lax.rem(z + d, n_exp)
-            held = is_end & (e == far)
-            if RELAY_BOTH:
-                held = held | (is_mid & (e == away))
-
-            @pl.when(~held)
+            @pl.when(~(is_end & (e == far)))
             def _():
-                ag_copy(g, z, e).start()
+                ag_copy(g, z, e, ag_send).start()
 
     for c in w_copies:
         c.wait()
@@ -341,8 +342,6 @@
             device_id_type=MESH,
         )
 
-    mine = pl.ds(pl.multiple_of(z * tok, tok), tok)
-
     def pass_on(before):
         earlier = pl.ds(before * per, per)
         rs_hop(before).wait_recv()
@@ -351,23 +350,25 @@
         part_out[earlier, part, :] = both.astype(jnp.bfloat16)
         rs_copy(before, lax.rem(away + n_exp - z, n_exp)).start()
 
+    def gathered(g):
+        arrived(rows.at[pl.ds(g * per, per), :, pl.ds(0, width - hd)], ag_recv.at[g]).wait_recv()
+
+    mine = pl.ds(pl.multiple_of(z * tok, tok), tok)
+
     @pl.loop(0, groups)
     def _(i):
         g = lax.rem(first_group + i, groups)
         members = pl.ds(g * per, per)
-        arrived(rows.at[members, :, pl.ds(0, width - hd)], ag_recv.at[g]).wait_recv()
+        gathered(g)
 
         @pl.when(is_mid)
         def _():
-            if RELAY_BOTH:
-                ag_copy(g, inner, near).start()
-            ag_copy(g, away, near).start()
+            ag_copy(g, away, near, far_send).start()
 
         x = rows[members].reshape(count, width).astype(jnp.float32)
         inv = 1.0 / jnp.sqrt(jnp.mean(x * x, axis=-1, keepdims=True) + 1e-06)
-        flat = (x * inv * gain_ref[...]).astype(jnp.bfloat16)
-        norm[members] = flat.reshape(per, local_len, width)
-        logits = lax.dot_general(
+        flat = (x * gain_ref[...]).astype(jnp.bfloat16)
+        logits = inv * lax.dot_general(
             flat, router_ref[...], (((1,), (1,)), ((), ())), preferred_element_type=jnp.float32
         )
         total = logits.shape[1]
@@ -381,29 +382,41 @@
         g0 = s0 * half
         g1 = s1 * half
         acc = None
-        for j in range(experts_here):
-            name = (z * experts_here + j).astype(jnp.float32)
-            gate = jnp.where(id0 == name, g0, 0.0) + jnp.where(id1 == name, g1, 0.0)
-            u = jnp.dot(flat, win[j], preferred_element_type=jnp.float32)
-            bent = jnp.tanh(u * (0.7978845608028654 + 0.035677408136300125 * (u * u)))
-            scaled = u * jnp.concatenate([gate] * (u.shape[1] // gate.shape[1]), axis=1)
-            t = jnp.dot(
-                (scaled + scaled * bent).astype(jnp.bfloat16), wout[j],
-                preferred_element_type=jnp.float32,
-            )
-            acc = t if acc is None else acc + t
+        for j in range(experts_here + AHEAD):
+            if j < experts_here:
+                name = (z * experts_here + j).astype(jnp.float32)
+                gate = jnp.where(id0 == name, g0, 0.0) + jnp.where(id1 == name, g1, 0.0)
+                gate = jnp.concatenate([gate * inv] * (CHUNK // gate.shape[1]), axis=1)
+                for c in range(0, hidden.shape[2], CHUNK):
+                    u = jnp.dot(flat, win[j, :, c:c + CHUNK], preferred_element_type=jnp.float32)
+                    scaled = u * gate
+                    u = u * inv
+                    bent = jnp.tanh(u * (0.7978845608028654 + 0.035677408136300125 * (u * u)))
+                    hidden[j, :, c:c + CHUNK] = (scaled + scaled * bent).astype(jnp.bfloat16)
+            if j >= AHEAD:
+                t = jnp.dot(
+                    hidden[j - AHEAD], wout[j - AHEAD], preferred_element_type=jnp.float32
+                )
+                acc = t if acc is None else acc + t
         acc = acc.reshape(per, local_len, width)
         part_out[members] = acc.astype(jnp.bfloat16)
         own_sum[members] = acc
-        direct = i >= groups - LAG
-
-        @pl.when(is_mid & (i >= LAG))
+        direct = i >= RELAYED
+
+        @pl.when(is_end & direct)
         def _():
-            pass_on(lax.rem(first_group + i + groups - LAG, groups))
+            rs_copy(g, lax.rem(far + n_exp - z, n_exp)).start()
 
         for d in range(1, n_exp):
             e = lax.rem(z + d, n_exp)
-            held = ~direct & ((is_end & (e == far)) | (is_mid & (e == away)))
+
+            @pl.when(is_end & (e != far) & (i == groups - 1))
+            def _():
+                rs_copy(lax.rem(g + groups - 1, groups), d).start()
+
+        for d in range(1, n_exp):
+            e = lax.rem(z + d, n_exp)
+            held = (is_end & ((e == far) | (i == groups - 2))) | (is_mid & ~direct & (e == away))
 
             @pl.when(~held)
             def _():
@@ -413,12 +426,19 @@
         def _():
             rs_hop(g).start()
 
-    normed_ref[...] = norm[:, mine, :]
+    @pl.when(is_mid)
+    def _():
+        for i in range(RELAYED):
+            pass_on(lax.rem(first_group + i, groups))
+
     for i in range(groups):
         g = lax.rem(first_group + i, groups)
         members = pl.ds(g * per, per)
+        x = rows[members, mine, :].astype(jnp.float32)
+        inv = 1.0 / jnp.sqrt(jnp.mean(x * x, axis=-1, keepdims=True) + 1e-06)
+        normed_ref[members] = (x * inv * gain_ref[...]).astype(jnp.bfloat16)
         acc = own_sum[members, mine, :]
-        if i >= groups - LAG:
+        if i >= RELAYED:
             arrived(part_in.at[pl.ds(0, n_exp - 1), members], rs_recv.at[g]).wait_recv()
         else:
             @pl.when(is_end)
@@ -445,7 +465,8 @@
 
     @pl.when(is_mid)
     def _():
-        sent(rows, ag_send)
+        sent(rows.at[:, :, pl.ds(0, (n_exp - 1) * hd)], ag_send)
+        sent(rows.at[:, :, pl.ds(0, hd)], far_send)
 
     @pl.when(~is_mid)
     def _():
@@ -491,16 +512,16 @@
             pltpu.VMEM((seq_len, hd), bf),
             pltpu.VMEM((seqs, local_len, width), bf),
             pltpu.VMEM((n_exp, seqs, TOPK, tok), jnp.int32),
-            pltpu.VMEM((seqs, local_len, width), bf),
             pltpu.VMEM((TOPK, groups, per * local_len, 128), f32),
             pltpu.VMEM((seqs, local_len, width), f32),
             pltpu.VMEM((seqs, local_len, width), bf),
             pltpu.VMEM((n_exp, seqs, tok, width), bf),
             pltpu.VMEM((seqs, tok, width), bf),
+            pltpu.VMEM((experts_here, per * local_len, ff), bf),
             pltpu.VMEM((experts_here, sub, ff), bf),
             pltpu.VMEM((experts_here, ff, sub), bf),
             dma((2,)), dma(()), dma((3,)), dma(()), dma(()), dma(()), dma((2,)), dma(()), dma((groups,)),
-            dma(()), dma((groups,)), dma(()), dma((groups,)), dma((groups,)),
+            dma(()), dma(()), dma((groups,)), dma(()), dma((groups,)), dma((groups,)),
         ],
         compiler_params=pltpu.CompilerParams(
             collective_id=0, has_side_effects=True, vmem_limit_bytes=60 * 1024 * 1024

time: 35.5 us -> 35.1 us (0.989)
  Pallas kernels: 34.8 us -> 34.3 us
    pallas_call x1, Pallas kernels: 34 us -> 33.6 us  [fused_body(): pl.pallas_call(functools.partial(fused_kernel, n_seq, n_exp, per), out_sh...]
where the time goes in v2:
time: 35.1 us; the launch traced here: 34.9 us
  Pallas kernels  34.3 us (98%)
  between operations  0.64 us (2%)
    pallas_call x1, Pallas kernels, fused_body(): pl.pallas_call(functools.partial(fused_kernel, n_seq, n_exp, per), out_sh...  33.6 us
    pallas_call x1, Pallas kernels, fused_body(): pl.pallas_call(move_kernel, out_shape=(result, result), in_specs=[pl.Bloc...  0.72 us

profile of v2, /device:TPU:0, one launch (start us, length us, event | category | flops | bytes accessed | tf_op | source)
XLA Modules:
  0.0 34.9 jit_solution(3325154926949054162)
XLA Ops:
  0.6 33.6 %shard_map.104 = (bf16[8,16,512]{2,1,0:T(8,128)(2,1)S(1)}, bf16[8,16,512]{2,1,0:T(8,128)(2,1)S(1)}) custom-call(bf16[8,64,128]{2,1,0:T(8,128)(2,1)} %q_ref.1, bf16[8,64,128]{2,1,0:T(8,128)(2,1)} %k_ref.1, bf16[8,64,128]{2,1,0:T(8,128)(2,1)} %v_ref.1, s32[8,512]{1,0:T(8,128)} %seg_hbm.1, f32[1,512]{1,0:T(1,128)} %bitcast.7, bf16[16,512]{1,0:T(8,128)(2,1)} %bitcast.5, ...), custom_call_target="tpu_custom_call" | custom-call | tf_op jit(solution)/shard_map/pallas_call | solution.py:499
  34.2 0.7 %shard_map.105 = (bf16[8,16,512]{2,1,0:T(8,128)(2,1)}, bf16[8,16,512]{2,1,0:T(8,128)(2,1)}) custom-call(bf16[8,16,512]{2,1,0:T(8,128)(2,1)S(1)} %get-tuple-element.4.a_ref, bf16[8,16,512]{2,1,0:T(8,128)(2,1)S(1)} %get-tuple-element.5.b_ref), custom_call_target="tpu_custom_call" | custom-call | tf_op jit(solution)/shard_map/pallas_call | solution.py:531

commit v3 on v2

--- a/solution.py
+++ b/solution.py
@@ -403,6 +403,10 @@
         own_sum[members] = acc
         direct = i >= RELAYED
 
+        @pl.when(is_end & ~direct)
+        def _():
+            rs_hop(g).start()
+
         @pl.when(is_end & direct)
         def _():
             rs_copy(g, lax.rem(far + n_exp - z, n_exp)).start()
@@ -421,10 +425,6 @@
             @pl.when(~held)
             def _():
                 rs_copy(g, d).start()
-
-        @pl.when(is_end & ~direct)
-        def _():
-            rs_hop(g).start()
 
     @pl.when(is_mid)
     def _():

time: 35.1 us -> 35.1 us (level)
  no operation moved by 1% of the time
where the time goes in v3:
time: 35.1 us; the launch traced here: 34.9 us
  Pallas kernels  34.3 us (98%)
  between operations  0.64 us (2%)
    pallas_call x1, Pallas kernels, fused_body(): pl.pallas_call(functools.partial(fused_kernel, n_seq, n_exp, per), out_sh...  33.6 us
    pallas_call x1, Pallas kernels, fused_body(): pl.pallas_call(move_kernel, out_shape=(result, result), in_specs=[pl.Bloc...  0.72 us

profile of v3, /device:TPU:0, one launch (start us, length us, event | category | flops | bytes accessed | tf_op | source)
XLA Modules:
  0.0 34.9 jit_solution(10759185107572708174)
XLA Ops:
  0.6 33.6 %shard_map.104 = (bf16[8,16,512]{2,1,0:T(8,128)(2,1)S(1)}, bf16[8,16,512]{2,1,0:T(8,128)(2,1)S(1)}) custom-call(bf16[8,64,128]{2,1,0:T(8,128)(2,1)} %q_ref.1, bf16[8,64,128]{2,1,0:T(8,128)(2,1)} %k_ref.1, bf16[8,64,128]{2,1,0:T(8,128)(2,1)} %v_ref.1, s32[8,512]{1,0:T(8,128)} %seg_hbm.1, f32[1,512]{1,0:T(1,128)} %bitcast.7, bf16[16,512]{1,0:T(8,128)(2,1)} %bitcast.5, ...), custom_call_target="tpu_custom_call" | custom-call | tf_op jit(solution)/shard_map/pallas_call | solution.py:499
  34.2 0.7 %shard_map.105 = (bf16[8,16,512]{2,1,0:T(8,128)(2,1)}, bf16[8,16,512]{2,1,0:T(8,128)(2,1)}) custom-call(bf16[8,16,512]{2,1,0:T(8,128)(2,1)S(1)} %get-tuple-element.4.a_ref, bf16[8,16,512]{2,1,0:T(8,128)(2,1)S(1)} %get-tuple-element.5.b_ref), custom_call_target="tpu_custom_call" | custom-call | tf_op jit(solution)/shard_map/pallas_call | solution.py:531
